TPU v7x, 32 devices: a whole 2x2x4 slice. The times are simulated.
32 devices in a mesh: dp: 2 (over x), expert: 16 (over z, y, core).
Axes of the slice: x: 2, y: 2, z: 4, core: 2. Of those that a mesh axis runs over, the one named last changes fastest.
Arguments:
- tokens: bfloat16 [4096, 1024], P(('dp', 'expert')), may hold values from -6 to 6
- out_grad: bfloat16 [4096, 1024], P(('dp', 'expert')), may hold values from -6 to 6
- expert_ids: int32 [4096, 3], P(('dp', 'expert')), may hold values from 0 to 15, all different within a row; in each aligned block of 128 rows (0 to 127, 128 to 255, ...) at most 30 rows name the same one
- gate_probs: float32 [4096, 3], P(('dp', 'expert')), may hold values from 0.1 to 0.6
- saved_pre: bfloat16 [2, 16, 480, 1536], P('dp', 'expert'), may hold values from -6 to 6
- gate_weight: bfloat16 [16, 1024, 768], P('expert', 'dp'), may hold values from -0.1875 to 0.1875
- up_weight: bfloat16 [16, 1024, 768], P('expert', 'dp'), may hold values from -0.1875 to 0.1875
- down_weight: bfloat16 [16, 1024, 768], P('expert', 'dp'), may hold values from -0.21875 to 0.21875
- basis: bfloat16 [16, 1024, 256], P('expert', 'dp'), may hold values from -0.1875 to 0.1875
Outputs:
- in_grad: bfloat16 [4096, 1024], P(('dp', 'expert'))
- proj_grads: float32 [16, 3, 256, 768], P('expert', None, 'dp')
Inputs may be any that keep to these rules, and one draw needn't show every extreme that they name: `expert_ids`: each token names 3 different experts. The rows of one device name one expert at most 30 times, and on some devices some expert exactly 30 times.
All inputs are finite; a program needn't handle non-finite values.
Results may differ from a plain program's by a relative error of at most 0.0091.
Values may be sent and summed in bfloat16 or wider, within the bound.
A program may use at most 64 MiB of HBM per device.

v0:
```python
import jax
import jax.numpy as jnp
from jax import lax
from jax.sharding import PartitionSpec as P


def contract_rows(left, right):
    return lax.dot_general(
        left, right, (((0,), (0,)), ((), ())), preferred_element_type=jnp.float32
    )


def contract_cols(left, right):
    return lax.dot_general(
        left, right, (((1,), (1,)), ((), ())), preferred_element_type=jnp.float32
    )


def body(
    tokens, out_grad, expert_ids, gate_probs, saved_pre, gate_weight, up_weight, down_weight, basis
):
    n_owner = lax.axis_size("expert")
    tok_rows, width = tokens.shape
    topk = expert_ids.shape[1]
    slots = saved_pre.shape[2]
    cap = slots // n_owner
    hidden = gate_weight.shape[2]
    onehot = (expert_ids[:, :, None] == jnp.arange(n_owner, dtype=jnp.int32)[None, None, :]).astype(
        jnp.int32
    )
    per_token = jnp.sum(onehot, axis=1)
    before = jnp.cumsum(per_token, axis=0) - per_token
    position = jnp.sum(onehot * before[:, None, :], axis=2)
    target = expert_ids * cap + position
    token_index = jnp.broadcast_to(jnp.arange(tok_rows, dtype=jnp.int32)[:, None], target.shape)
    choice_index = jnp.broadcast_to(jnp.arange(topk, dtype=jnp.int32)[None, :], target.shape)
    fill_token = (
        jnp.full((n_owner * cap,), -1, jnp.int32)
        .at[target.reshape(-1)]
        .set(token_index.reshape(-1))
    )
    fill_choice = (
        jnp.zeros((n_owner * cap,), jnp.int32).at[target.reshape(-1)].set(choice_index.reshape(-1))
    )
    filled = fill_token >= 0
    picked = jnp.maximum(fill_token, 0)
    send_rows = jnp.where(filled[:, None], tokens[picked], jnp.zeros((), jnp.bfloat16))
    weight_pick = gate_probs[picked, fill_choice]
    scaled = (out_grad[picked].astype(jnp.float32) * weight_pick[:, None]).astype(jnp.bfloat16)
    send_grad = jnp.where(filled[:, None], scaled, jnp.zeros((), jnp.bfloat16))
    arrived_rows, arrived_grad = (
        lax.all_to_all(
            send_rows.reshape(n_owner, cap, width),
            "expert",
            split_axis=0,
            concat_axis=0,
            tiled=True,
        ),
        lax.all_to_all(
            send_grad.reshape(n_owner, cap, width),
            "expert",
            split_axis=0,
            concat_axis=0,
            tiled=True,
        ),
    )
    rows_in = arrived_rows.reshape(slots, width)
    grad_in = arrived_grad.reshape(slots, width)
    pieces = (
        lax.all_gather(down_weight, "dp", axis=1, tiled=True),
        lax.all_gather(basis, "dp", axis=1, tiled=True),
    )
    down_piece = pieces[0][0]
    basis_piece = pieces[1][0]
    hidden_grad = jnp.dot(grad_in, down_piece, preferred_element_type=jnp.float32)
    x_acc = jnp.dot(rows_in, basis_piece, preferred_element_type=jnp.float32)
    dy_acc = jnp.dot(grad_in, basis_piece, preferred_element_type=jnp.float32)
    hidden_grad, x_acc, dy_acc = (hidden_grad, x_acc, dy_acc)
    pre = saved_pre[0, 0].astype(jnp.float32)
    gate_pre = pre[:, :hidden]
    up_pre = pre[:, hidden:]
    sig = jax.nn.sigmoid(gate_pre)
    hid = (gate_pre * sig * up_pre).astype(jnp.bfloat16)
    up_grad = (hidden_grad * gate_pre * sig).astype(jnp.bfloat16)
    gate_grad = (hidden_grad * up_pre * sig * (1.0 + gate_pre * (1.0 - sig))).astype(jnp.bfloat16)
    x_proj = x_acc.astype(jnp.bfloat16)
    dy_proj = dy_acc.astype(jnp.bfloat16)
    pieces = lax.all_gather((gate_weight, up_weight), "dp", axis=1, tiled=True)
    row_grad = contract_cols(gate_grad, pieces[0][0]) + contract_cols(up_grad, pieces[1][0])
    terms = jnp.stack(
        [
            contract_rows(x_proj, gate_grad),
            contract_rows(x_proj, up_grad),
            contract_rows(dy_proj, hid),
        ]
    )
    proj_grads = lax.psum_scatter(terms[None], "dp", scatter_dimension=2, tiled=True)
    returned = lax.all_to_all(
        row_grad.astype(jnp.bfloat16).reshape(n_owner, cap, width),
        "expert",
        split_axis=0,
        concat_axis=0,
        tiled=True,
    )
    returned = returned.reshape(n_owner * cap, width)
    in_grad = jnp.sum(returned[target].astype(jnp.float32), axis=1).astype(jnp.bfloat16)
    return (in_grad, proj_grads)


def solution(mesh):
    return jax.shard_map(
        body,
        mesh=mesh,
        in_specs=(
            P(("dp", "expert"), None),
            P(("dp", "expert"), None),
            P(("dp", "expert"), None),
            P(("dp", "expert"), None),
            P("dp", "expert", None, None),
            P("expert", "dp", None),
            P("expert", "dp", None),
            P("expert", "dp", None),
            P("expert", "dp", None),
        ),
        out_specs=(P(("dp", "expert"), None), P("expert", None, "dp", None)),
        check_vma=False,
    )
```

profile of v0, /device:TPU:11, one launch (start us, length us, event | category | flops | bytes accessed | tf_op | source)
XLA Modules:
  0.0 154.2 jit_solution(18222967836924440757)
XLA Ops:
  7.2 0.7 all-gather.4.cloned.1.call-update
  7.9 0.7 convert_reduce_fusion
  8.6 0.1 copy.15
  8.7 0.2 reduce_window_sum.11
  8.9 0.7 select_reduce_fusion
  9.7 0.7 compare_select_fusion.1
  10.4 0.1 copy.18
  10.5 0.2 reshape.88
  10.7 0.2 reshape.131
  10.9 0.2 reshape.139
  11.1 2.9 %scatter_custom_fusion.1 = s32[480]{0:T(512)S(1)} fusion(s32[384]{0:T(512)S(1)} %fusion.12, s32[384]{0:T(512)S(1)} %reshape.139, s32[]{:T(128)} %constant.9.clone.1), kind=kCustom, calls=%fused_computation.41 | custom fusion | bytes 1924 | tf_op jit(solution)/shard_map/scatter | solution.py:43
  14.1 2.9 %scatter_custom_fusion = s32[480]{0:T(512)S(1)} fusion(s32[384]{0:T(512)S(1)} %fusion.12, s32[384]{0:T(512)S(1)} %reshape.131, s32[]{:T(128)} %constant.7.clone.1), kind=kCustom, calls=%fused_computation.45 | custom fusion | bytes 1924 | tf_op jit(solution)/shard_map/scatter | solution.py:40
  17.0 2.8 %gather_fusion = bf16[480,1024]{1,0:T(8,128)(2,1)} fusion(bf16[128,1024]{1,0:T(8,128)(2,1)S(1)} %copy-done, s32[1024]{0:T(1024)S(1)} %pad_clamp_fusion.1), kind=kCustom, calls=%fused_computation | custom fusion | bytes 1968000 | tf_op jit(solution)/shard_map/gather | solution.py:49
  19.8 1.5 reshape.95
  21.3 2.8 %gather_fusion.3 = bf16[480,1024]{1,0:T(8,128)(2,1)} fusion(bf16[128,1024]{1,0:T(8,128)(2,1)S(1)} %copy-done.2, s32[1024]{0:T(1024)S(1)} %pad_clamp_fusion.1), kind=kCustom, calls=%fused_computation.3 | custom fusion | bytes 1968000 | tf_op jit(solution)/shard_map/gather | solution.py:47
  24.1 1.4 gather.18
  25.5 4.6 %gather_fusion.1 = f32[480]{0:T(512)S(1)} fusion(f32[128,3]{0,1:T(4,128)S(1)} %copy-done.1, s32[480]{0:T(512)S(1)} %get-tuple-element.8), kind=kCustom, calls=%fused_computation.1 | custom fusion | bytes 7680 | tf_op jit(solution)/shard_map/gather | solution.py:48
  30.3 0.1 broadcast_in_dim.57
  30.3 1.7 %broadcast_select_fusion = (bf16[16,30,1024]{2,1,0:T(8,128)(2,1)}, bf16[16,30,1024]{2,1,0:T(8,128)(2,1)}) fusion(bf16[16,30,1024]{2,1,0:T(8,128)(2,1)S(1)} %gather.18, pred[16,30]{1,0:T(8,128)(4,1)S(1)} %broadcast_in_dim.57, f32[16,30,1024]{2,1,0:T(8,128)S(1)} %reshape.95, f32[16,30]{1,0:T(8,128)S(1)} %mul.53), kind=kLoop, calls=%fused_computation.25 | loop fusion | flops 1966080 | bytes 4917600 | tf_op jit(solution)/shard_map/jit(_where)/select_n | solution.py:47
  32.0 6.5 %all-to-all-start.2 = ((bf16[16,30,1024]{2,1,0:T(8,128)(2,1)}), bf16[16,30,1024]{2,1,0:T(8,128)(2,1)S(1)}, u32[]{:S(2)}, u32[]{:S(2)}) async-start(bf16[16,30,1024]{2,1,0:T(8,128)(2,1)} %get-tuple-element.6), calls=%async_computation.2 | async-start | bytes 2097152 | tf_op jit(solution)/shard_map/all_to_all | solution.py:52
  38.6 0.7 all-gather.6.cloned.1.call-update
  39.3 24.2 %all-to-all-done.2 = bf16[16,30,1024]{2,1,0:T(8,128)(2,1)S(1)} async-done(((bf16[16,30,1024]{2,1,0:T(8,128)(2,1)}), bf16[16,30,1024]{2,1,0:T(8,128)(2,1)S(1)}, u32[]{:S(2)}, u32[]{:S(2)}) %all-to-all-start.2) | async-done | bytes 983072 | tf_op jit(solution)/shard_map/all_to_all | solution.py:52
  63.5 4.7 %all-to-all-start = ((bf16[16,30,1024]{2,1,0:T(8,128)(2,1)}), bf16[16,30,1024]{2,1,0:T(8,128)(2,1)S(1)}, u32[]{:S(2)}, u32[]{:S(2)}) async-start(bf16[16,30,1024]{2,1,0:T(8,128)(2,1)} %get-tuple-element.7), calls=%async_computation | async-start | bytes 2097152 | tf_op jit(solution)/shard_map/all_to_all | solution.py:59
  68.3 0.7 all-gather.8.cloned.1.call-update
  69.0 8.3 %all_gather.15 = bf16[1,1024,256]{2,1,0:T(8,128)(2,1)S(1)} all-gather(bf16[1,512,256]{2,1,0:T(8,128)(2,1)S(1)} %copy-done.7), channel_id=1, replica_groups=mesh['dp'=2,'expert'=16] {'dp'}, dimensions={1}, use_global_device_ids=true | all-gather | bytes 786432 | tf_op jit(solution)/shard_map/all_gather | solution.py:71
  77.4 3.7 %bitcast_convert_fusion = f32[480,1536]{1,0:T(8,128)} fusion(bf16[1,1,480,1536]{3,2,1,0:T(8,128)(2,1)} %param.13), kind=kLoop, calls=%fused_computation.14 | loop fusion | flops 737280 | bytes 4423680 | tf_op jit(solution)/shard_map/convert_element_type | solution.py:79
  81.0 1.2 reshape.94
  82.2 1.6 %convolution_convert_fusion.1 = bf16[480,256]{1,0:T(8,128)(2,1)S(1)} fusion(bf16[480,1024]{1,0:T(8,128)(2,1)} %reshape.94, bf16[1,1024,256]{2,1,0:T(8,128)(2,1)S(1)} %all_gather.15), kind=kOutput, calls=%fused_computation.23 | convolution fusion | flops 251781120 | bytes 1753088 | tf_op jit(solution)/shard_map/dot_general | solution.py:76
  83.8 9.4 %all-to-all-done = bf16[16,30,1024]{2,1,0:T(8,128)(2,1)S(1)} async-done(((bf16[16,30,1024]{2,1,0:T(8,128)(2,1)}), bf16[16,30,1024]{2,1,0:T(8,128)(2,1)S(1)}, u32[]{:S(2)}, u32[]{:S(2)}) %all-to-all-start) | async-done | bytes 983072 | tf_op jit(solution)/shard_map/all_to_all | solution.py:59
  93.2 0.3 reshape.91
  93.5 3.8 %multiply_convert_fusion.2 = (bf16[480,768]{1,0:T(8,128)(2,1)S(1)}, bf16[480,768]{1,0:T(8,128)(2,1)S(1)}) fusion(f32[480,1536]{1,0:T(8,128)} %bitcast_convert_fusion, bf16[480,1024]{1,0:T(8,128)(2,1)S(1)} %reshape.91, bf16[1,1024,768]{2,1,0:T(8,128)(2,1)} %all-gather.4.cloned.1.call-done), kind=kOutput, calls=%fused_computation.16 | convolution fusion | flops 759767040 | bytes 6979584 | tf_op jit(solution)/shard_map/dot_general | solution.py:75
  97.4 0.4 convolution_bitcast_fusion.2
  97.8 0.5 copy-done.4
  98.3 0.4 convolution_bitcast_fusion.1
  98.7 3.4 %convolution_bitcast_fusion = f32[1,256,768]{2,1,0:T(8,128)S(1)} fusion(bf16[480,1024]{1,0:T(8,128)(2,1)} %copy-done.3, f32[480,1536]{1,0:T(8,128)} %bitcast_convert_fusion, bf16[1,1024,256]{2,1,0:T(8,128)(2,1)} %copy-done.6), kind=kOutput, calls=%fused_computation.19 | convolution fusion | flops 442736640 | bytes 5242880 | tf_op jit(solution)/shard_map/dot_general | solution.py:8
  102.1 1.6 %maximum_bitcast_fusion = f32[1,3,256,768]{3,2,1,0:T(8,128)} fusion(f32[1,256,768]{2,1,0:T(8,128)S(1)} %convolution_bitcast_fusion, f32[1,256,768]{2,1,0:T(8,128)S(1)} %convolution_bitcast_fusion.1, f32[1,256,768]{2,1,0:T(8,128)S(1)} %convolution_bitcast_fusion.2), kind=kLoop, calls=%fused_computation.6 | loop fusion | flops 1179648 | bytes 4718592 | tf_op jit(solution)/shard_map/broadcast_in_dim | solution.py:97
  103.8 1.1 copy-done.5
  104.8 3.7 %fusion.1 = f32[480,1024]{1,0:T(8,128)} fusion(bf16[480,768]{1,0:T(8,128)(2,1)S(1)} %copy-done.5, bf16[1,1024,768]{2,1,0:T(8,128)(2,1)} %all-gather.6.cloned.1.call-done), kind=kOutput, calls=%fused_computation.10 | convolution fusion | flops 754974720 | bytes 4276224 | tf_op jit(solution)/shard_map/dot_general | solution.py:14
  108.5 3.6 %add_convert_fusion = bf16[480,1024]{1,0:T(8,128)(2,1)S(1)} fusion(f32[480,1024]{1,0:T(8,128)} %fusion.1, bf16[480,768]{1,0:T(8,128)(2,1)S(1)} %get-tuple-element.4, bf16[1,1024,768]{2,1,0:T(8,128)(2,1)} %all-gather.8.cloned.1.call-done), kind=kOutput, calls=%fused_computation.8 | convolution fusion | flops 755957760 | bytes 5259264 | tf_op jit(solution)/shard_map/dot_general | solution.py:14
  112.1 1.2 reshape.92
  113.4 4.5 %all-to-all-start.1 = ((bf16[16,30,1024]{2,1,0:T(8,128)(2,1)}), bf16[16,30,1024]{2,1,0:T(8,128)(2,1)S(1)}, u32[]{:S(2)}, u32[]{:S(2)}) async-start(bf16[16,30,1024]{2,1,0:T(8,128)(2,1)} %reshape.92), calls=%async_computation.1 | async-start | bytes 2097152 | tf_op jit(solution)/shard_map/all_to_all | solution.py:98
  117.8 0.1 copy.19
  117.9 0.2 reshape.113
  118.2 24.6 %all-to-all-done.1 = bf16[16,30,1024]{2,1,0:T(8,128)(2,1)S(1)} async-done(((bf16[16,30,1024]{2,1,0:T(8,128)(2,1)}), bf16[16,30,1024]{2,1,0:T(8,128)(2,1)S(1)}, u32[]{:S(2)}, u32[]{:S(2)}) %all-to-all-start.1) | async-done | bytes 983072 | tf_op jit(solution)/shard_map/all_to_all | solution.py:98
  142.8 0.3 reshape.93
  143.0 2.1 %gather_fusion.2 = bf16[384,1024]{1,0:T(8,128)(2,1)S(1)} fusion(bf16[480,1024]{1,0:T(8,128)(2,1)S(1)} %reshape.93, s32[1024]{0:T(1024)S(1)} %pad_clamp_fusion), kind=kCustom, calls=%fused_computation.2 | custom fusion | bytes 1574400 | tf_op jit(solution)/shard_map/gather | solution.py:106
  145.1 0.5 reshape.116
  145.6 2.1 %reduce_sum.32 = bf16[128,1024]{1,0:T(8,128)(2,1)} reduce(bf16[128,3,1024]{2,1,0:T(4,128)(2,1)S(1)} %reshape.116, bf16[]{:T(256)} %constant.12.clone.1), dimensions={1}, to_apply=%region_5.6 | reduce | flops 262144 | bytes 1048578 | tf_op jit(solution)/shard_map/reduce_sum | solution.py:106
  (33 shorter events, 0.5 us)
Async XLA Ops:
  7.2 9.9 %copy-start = (bf16[128,1024]{1,0:T(8,128)(2,1)S(1)}, bf16[128,1024]{1,0:T(8,128)(2,1)}, u32[]{:S(2)}) copy-start(bf16[128,1024]{1,0:T(8,128)(2,1)} %param.10) | copy-start | bytes 786436
  7.2 86.3 %all-gather.4.cloned.1.call-start = ((), (), s32[]{:S(2)}) async-start(), calls=%async_computation.4 | async-start | bytes 2359296 | tf_op jit(solution)/shard_map/all_gather | solution.py:70
  19.8 1.5 copy-start.2
  24.1 1.5 copy-start.1
  32.0 31.5 %all-to-all-start.2 = ((bf16[16,30,1024]{2,1,0:T(8,128)(2,1)}), bf16[16,30,1024]{2,1,0:T(8,128)(2,1)S(1)}, u32[]{:S(2)}, u32[]{:S(2)}) async-start(bf16[16,30,1024]{2,1,0:T(8,128)(2,1)} %get-tuple-element.6), calls=%async_computation.2 | async-start | bytes 2097152 | tf_op jit(solution)/shard_map/all_to_all | solution.py:52
  38.6 65.2 %all-gather.6.cloned.1.call-start = ((), (), s32[]{:S(2)}) async-start(), calls=%async_computation.5 | async-start | bytes 2359296 | tf_op jit(solution)/shard_map/all_gather | solution.py:88
  39.3 29.7 %copy-start.7 = (bf16[1,512,256]{2,1,0:T(8,128)(2,1)S(1)}, bf16[1,512,256]{2,1,0:T(8,128)(2,1)}, u32[]{:S(2)}) copy-start(bf16[1,512,256]{2,1,0:T(8,128)(2,1)} %param.17) | copy-start | bytes 786436
  63.5 29.7 %all-to-all-start = ((bf16[16,30,1024]{2,1,0:T(8,128)(2,1)}), bf16[16,30,1024]{2,1,0:T(8,128)(2,1)S(1)}, u32[]{:S(2)}, u32[]{:S(2)}) async-start(bf16[16,30,1024]{2,1,0:T(8,128)(2,1)} %get-tuple-element.7), calls=%async_computation | async-start | bytes 2097152 | tf_op jit(solution)/shard_map/all_to_all | solution.py:59
  68.2 40.2 %all-gather.8.cloned.1.call-start = ((), (), s32[]{:S(2)}) async-start(), calls=%async_computation.6 | async-start | bytes 2359296 | tf_op jit(solution)/shard_map/all_gather | solution.py:88
  69.0 78.7 %reduce-scatter.2.cloned.1.call-start = ((), (), s32[]{:S(2)}) async-start(), calls=%async_computation.7 | async-start | bytes 3538944 | tf_op jit(solution)/shard_map/reduce_scatter | solution.py:97
  77.3 4.9 %copy-start.6 = (bf16[1,1024,256]{2,1,0:T(8,128)(2,1)}, bf16[1,1024,256]{2,1,0:T(8,128)(2,1)S(1)}, u32[]{:S(2)}) copy-start(bf16[1,1024,256]{2,1,0:T(8,128)(2,1)S(1)} %all_gather.15) | copy-start | bytes 1572868
  93.5 3.9 %copy-start.3 = (bf16[480,1024]{1,0:T(8,128)(2,1)}, bf16[480,1024]{1,0:T(8,128)(2,1)S(1)}, u32[]{:S(2)}) copy-start(bf16[480,1024]{1,0:T(8,128)(2,1)S(1)} %reshape.91) | copy-start | bytes 2949124
  97.4 0.9 copy-start.4
  103.7 1.1 copy-start.5
  113.4 29.4 %all-to-all-start.1 = ((bf16[16,30,1024]{2,1,0:T(8,128)(2,1)}), bf16[16,30,1024]{2,1,0:T(8,128)(2,1)S(1)}, u32[]{:S(2)}, u32[]{:S(2)}) async-start(bf16[16,30,1024]{2,1,0:T(8,128)(2,1)} %reshape.92), calls=%async_computation.1 | async-start | bytes 2097152 | tf_op jit(solution)/shard_map/all_to_all | solution.py:98
Sparse Core Ops, SparseCore 0:
  9.5 27.2 all-gather.3
  40.9 26.6 all-gather.5
  70.6 26.6 all-gather.7
  103.9 33.0 reduce-scatter.1
where the time goes:
time: 155 us; the launch traced here: 154 us
  waiting for transfers between devices  60.3 us (39%)
  local copies, waits for them, and re-layouts  27.4 us (18%)
  matrix products  16.9 us (11%)
  starting transfers between devices  15.8 us (10%)
  between operations  14 us (9%)
  other arithmetic  11.4 us (7%)
  blocking collectives  8.31 us (5%)
    all_to_all x1, waiting for transfers between devices, body(): lax.all_to_all(row_grad.astype(jnp.bfloat16).reshape(n_owner, cap, width)...  24.6 us
    all_to_all x1, waiting for transfers between devices, body(): lax.all_to_all(send_rows.reshape(n_owner, cap, width), 'expert', split_ax...  24.2 us
    all_to_all x1, waiting for transfers between devices, body(): lax.all_to_all(send_grad.reshape(n_owner, cap, width), 'expert', split_ax...  9.38 us
    all_gather x1, blocking collectives, body(): lax.all_gather(basis, 'dp', axis=1, tiled=True)  8.31 us
    dot_general x2, matrix products, contract_cols(): lax.dot_general(left, right, (((1,), (1,)), ((), ())), preferred_element_...  7.29 us
    all_to_all x1, starting transfers between devices, body(): lax.all_to_all(send_rows.reshape(n_owner, cap, width), 'expert', split_ax...  6.52 us
    all_to_all x1, starting transfers between devices, body(): lax.all_to_all(send_grad.reshape(n_owner, cap, width), 'expert', split_ax...  4.7 us
    gather x1, local copies, waits for them, and re-layouts, body(): weight_pick = gate_probs[picked, fill_choice]  4.64 us
  transfers between devices with their start and end apart: 7, of which 3 were waited for; matrix products, arithmetic and copies ran while one was open for 35% of the time, Pallas kernels for 0%

commit v1 on v0

--- a/solution.py
+++ b/solution.py
@@ -2,6 +2,18 @@
 import jax.numpy as jnp
 from jax import lax
 from jax.sharding import PartitionSpec as P
+
+
+def gather_by_bits(array, axis, dim):
+    ways, here, step = (lax.axis_size(axis), lax.axis_index(axis), array.shape[dim])
+    line, have = (array, 1)
+    while have < ways:
+        line = jnp.concatenate(
+            [line, lax.ppermute(line, axis, [(d, (d - have) % ways) for d in range(ways)])],
+            axis=dim,
+        )
+        have = 2 * have
+    return jnp.roll(line, here * step, axis=dim)
 
 
 def contract_rows(left, right):
@@ -66,10 +78,7 @@
     )
     rows_in = arrived_rows.reshape(slots, width)
     grad_in = arrived_grad.reshape(slots, width)
-    pieces = (
-        lax.all_gather(down_weight, "dp", axis=1, tiled=True),
-        lax.all_gather(basis, "dp", axis=1, tiled=True),
-    )
+    pieces = (lax.all_gather(down_weight, "dp", axis=1, tiled=True), gather_by_bits(basis, "dp", 1))
     down_piece = pieces[0][0]
     basis_piece = pieces[1][0]
     hidden_grad = jnp.dot(grad_in, down_piece, preferred_element_type=jnp.float32)

time: 155 us -> 155 us (level)
  blocking collectives: 8.31 us -> 0 us
  waiting for transfers between devices: 60.3 us -> 65.9 us
  other arithmetic: 11.4 us -> 13.4 us
    all_gather x1 -> x0, blocking collectives: 8.31 us -> none  [body(): lax.all_gather(basis, 'dp', axis=1, tiled=True)]
    ppermute x0 -> x1, waiting for transfers between devices: none -> 3.36 us  [gather_by_bits(): lax.ppermute(line, axis, [(d, (d - have) % ways) for d in range(ways)])]
    all_to_all x1, waiting for transfers between devices: 9.38 us -> 11.9 us  [body(): lax.all_to_all(send_grad.reshape(n_owner, cap, width), 'expert', split_ax...]
    squeeze x0 -> x1, other arithmetic: none -> 2.41 us  [body(): basis_piece = pieces[1][0]]
  transfers between devices with their start and end apart: 7 -> 8, of which waited for: 3 -> 4; matrix products, arithmetic and copies ran while one was open for 35% -> 36% of each run, Pallas kernels for 0% -> 0%
where the time goes in v1:
time: 155 us; the launch traced here: 154 us
  waiting for transfers between devices  65.9 us (43%)
  local copies, waits for them, and re-layouts  27.4 us (18%)
  matrix products  17 us (11%)
  starting transfers between devices  16.4 us (11%)
  between operations  14 us (9%)
  other arithmetic  13.4 us (9%)
    all_to_all x1, waiting for transfers between devices, body(): lax.all_to_all(row_grad.astype(jnp.bfloat16).reshape(n_owner, cap, width)...  24.6 us
    all_to_all x1, waiting for transfers between devices, body(): lax.all_to_all(send_rows.reshape(n_owner, cap, width), 'expert', split_ax...  24.2 us
    all_to_all x1, waiting for transfers between devices, body(): lax.all_to_all(send_grad.reshape(n_owner, cap, width), 'expert', split_ax...  11.9 us
    dot_general x2, matrix products, contract_cols(): lax.dot_general(left, right, (((1,), (1,)), ((), ())), preferred_element_...  7.28 us
    all_to_all x1, starting transfers between devices, body(): lax.all_to_all(send_rows.reshape(n_owner, cap, width), 'expert', split_ax...  6.52 us
    all_to_all x1, starting transfers between devices, body(): lax.all_to_all(send_grad.reshape(n_owner, cap, width), 'expert', split_ax...  4.7 us
    gather x1, local copies, waits for them, and re-layouts, body(): weight_pick = gate_probs[picked, fill_choice]  4.64 us
    all_to_all x1, starting transfers between devices, body(): lax.all_to_all(row_grad.astype(jnp.bfloat16).reshape(n_owner, cap, width)...  4.48 us
  transfers between devices with their start and end apart: 8, of which 4 were waited for; matrix products, arithmetic and copies ran while one was open for 36% of the time, Pallas kernels for 0%

profile of v1, /device:TPU:11, one launch (start us, length us, event | category | flops | bytes accessed | tf_op | source)
XLA Modules:
  0.0 154.0 jit_solution(10189750230395397855)
XLA Ops:
  7.2 0.7 all-gather.4.cloned.1.call-update
  7.9 0.7 convert_reduce_fusion
  8.7 0.2 reduce_window_sum.11
  8.9 0.7 select_reduce_fusion
  9.7 0.7 compare_select_fusion.1
  10.4 0.1 copy.18
  10.5 0.2 reshape.88
  10.7 0.2 reshape.131
  10.9 0.2 reshape.139
  11.1 2.9 %scatter_custom_fusion.1 = s32[480]{0:T(512)S(1)} fusion(s32[384]{0:T(512)S(1)} %fusion.13, s32[384]{0:T(512)S(1)} %reshape.139, s32[]{:T(128)} %constant.44.clone.1), kind=kCustom, calls=%fused_computation.47 | custom fusion | bytes 1924 | tf_op jit(solution)/shard_map/scatter | solution.py:55
  14.1 2.9 %scatter_custom_fusion = s32[480]{0:T(512)S(1)} fusion(s32[384]{0:T(512)S(1)} %fusion.13, s32[384]{0:T(512)S(1)} %reshape.131, s32[]{:T(128)} %constant.21.clone.1), kind=kCustom, calls=%fused_computation.51 | custom fusion | bytes 1924 | tf_op jit(solution)/shard_map/scatter | solution.py:52
  17.0 2.8 %gather_fusion = bf16[480,1024]{1,0:T(8,128)(2,1)} fusion(bf16[128,1024]{1,0:T(8,128)(2,1)S(1)} %copy-done, s32[1024]{0:T(1024)S(1)} %pad_clamp_fusion.1), kind=kCustom, calls=%fused_computation | custom fusion | bytes 1968000 | tf_op jit(solution)/shard_map/gather | solution.py:61
  19.8 1.5 reshape.95
  21.3 2.8 %gather_fusion.3 = bf16[480,1024]{1,0:T(8,128)(2,1)} fusion(bf16[128,1024]{1,0:T(8,128)(2,1)S(1)} %copy-done.2, s32[1024]{0:T(1024)S(1)} %pad_clamp_fusion.1), kind=kCustom, calls=%fused_computation.3 | custom fusion | bytes 1968000 | tf_op jit(solution)/shard_map/gather | solution.py:59
  24.1 1.4 gather.18
  25.5 4.6 %gather_fusion.1 = f32[480]{0:T(512)S(1)} fusion(f32[128,3]{0,1:T(4,128)S(1)} %copy-done.1, s32[480]{0:T(512)S(1)} %get-tuple-element.8), kind=kCustom, calls=%fused_computation.1 | custom fusion | bytes 7680 | tf_op jit(solution)/shard_map/gather | solution.py:60
  30.3 1.6 %broadcast_select_fusion = (bf16[16,30,1024]{2,1,0:T(8,128)(2,1)}, bf16[16,30,1024]{2,1,0:T(8,128)(2,1)}) fusion(bf16[16,30,1024]{2,1,0:T(8,128)(2,1)S(1)} %gather.18, pred[16,30]{1,0:T(8,128)(4,1)S(1)} %broadcast_in_dim.57, f32[16,30,1024]{2,1,0:T(8,128)S(1)} %reshape.95, f32[16,30]{1,0:T(8,128)S(1)} %mul.56), kind=kLoop, calls=%fused_computation.29 | loop fusion | flops 1966080 | bytes 4917600 | tf_op jit(solution)/shard_map/jit(_where)/select_n | solution.py:59
  31.9 6.5 %all-to-all-start.2 = ((bf16[16,30,1024]{2,1,0:T(8,128)(2,1)}), bf16[16,30,1024]{2,1,0:T(8,128)(2,1)S(1)}, u32[]{:S(2)}, u32[]{:S(2)}) async-start(bf16[16,30,1024]{2,1,0:T(8,128)(2,1)} %get-tuple-element.6), calls=%async_computation.2 | async-start | bytes 2097152 | tf_op jit(solution)/shard_map/all_to_all | solution.py:64
  38.5 0.7 all-gather.6.cloned.1.call-update
  39.2 24.2 %all-to-all-done.2 = bf16[16,30,1024]{2,1,0:T(8,128)(2,1)S(1)} async-done(((bf16[16,30,1024]{2,1,0:T(8,128)(2,1)}), bf16[16,30,1024]{2,1,0:T(8,128)(2,1)S(1)}, u32[]{:S(2)}, u32[]{:S(2)}) %all-to-all-start.2) | async-done | bytes 983072 | tf_op jit(solution)/shard_map/all_to_all | solution.py:64
  63.4 4.7 %all-to-all-start = ((bf16[16,30,1024]{2,1,0:T(8,128)(2,1)}), bf16[16,30,1024]{2,1,0:T(8,128)(2,1)S(1)}, u32[]{:S(2)}, u32[]{:S(2)}) async-start(bf16[16,30,1024]{2,1,0:T(8,128)(2,1)} %get-tuple-element.7), calls=%async_computation | async-start | bytes 2097152 | tf_op jit(solution)/shard_map/all_to_all | solution.py:71
  68.2 0.3 collective-permute-start
  68.5 0.4 all-gather.8.cloned.1.call-update
  68.9 0.2 reduce-scatter.2.cloned.1.call-start
  69.1 3.4 %bitcast_convert_fusion = f32[480,1536]{1,0:T(8,128)} fusion(bf16[1,1,480,1536]{3,2,1,0:T(8,128)(2,1)} %param.13), kind=kLoop, calls=%fused_computation.14 | loop fusion | flops 737280 | bytes 4423680 | tf_op jit(solution)/shard_map/convert_element_type | solution.py:88
  72.5 3.4 %collective-permute-done = bf16[1,512,256]{2,1,0:T(8,128)(2,1)} collective-permute-done((bf16[1,512,256]{2,1,0:T(8,128)(2,1)S(1)}, bf16[1,512,256]{2,1,0:T(8,128)(2,1)}, u32[]{:S(2)}, u32[]{:S(2)}) %collective-permute-start) | collective-permute-done | bytes 262176 | tf_op jit(solution)/shard_map/ppermute | solution.py:12
  75.8 2.4 %fusion.9 = bf16[1024,256]{1,0:T(8,128)(2,1)S(1)} fusion(s32[]{:T(128)S(6)} %select_n.48, bf16[1,512,256]{2,1,0:T(8,128)(2,1)S(1)} %copy-done.7, bf16[1,512,256]{2,1,0:T(8,128)(2,1)} %collective-permute-done), kind=kLoop, calls=%fused_computation.33 | loop fusion | flops 2097152 | bytes 1048580 | tf_op jit(solution)/shard_map/squeeze | solution.py:83
  78.3 1.2 reshape.94
  79.5 1.7 %convolution_convert_fusion.1 = bf16[480,256]{1,0:T(8,128)(2,1)S(1)} fusion(bf16[480,1024]{1,0:T(8,128)(2,1)} %reshape.94, bf16[1024,256]{1,0:T(8,128)(2,1)S(1)} %fusion.9), kind=kOutput, calls=%fused_computation.23 | convolution fusion | flops 251781120 | bytes 1753088 | tf_op jit(solution)/shard_map/dot_general | solution.py:85
  81.2 11.9 %all-to-all-done = bf16[16,30,1024]{2,1,0:T(8,128)(2,1)S(1)} async-done(((bf16[16,30,1024]{2,1,0:T(8,128)(2,1)}), bf16[16,30,1024]{2,1,0:T(8,128)(2,1)S(1)}, u32[]{:S(2)}, u32[]{:S(2)}) %all-to-all-start) | async-done | bytes 983072 | tf_op jit(solution)/shard_map/all_to_all | solution.py:71
  93.1 0.3 reshape.91
  93.4 3.8 %multiply_convert_fusion.2 = (bf16[480,768]{1,0:T(8,128)(2,1)S(1)}, bf16[480,768]{1,0:T(8,128)(2,1)S(1)}) fusion(f32[480,1536]{1,0:T(8,128)} %bitcast_convert_fusion, bf16[480,1024]{1,0:T(8,128)(2,1)S(1)} %reshape.91, bf16[1,1024,768]{2,1,0:T(8,128)(2,1)} %all-gather.4.cloned.1.call-done), kind=kOutput, calls=%fused_computation.16 | convolution fusion | flops 759767040 | bytes 6979584 | tf_op jit(solution)/shard_map/dot_general | solution.py:84
  97.3 0.4 convolution_bitcast_fusion.2
  97.7 0.5 copy-done.4
  98.1 0.4 convolution_bitcast_fusion.1
  98.5 3.4 %convolution_bitcast_fusion = f32[1,256,768]{2,1,0:T(8,128)S(1)} fusion(bf16[480,1024]{1,0:T(8,128)(2,1)} %copy-done.3, bf16[1024,256]{1,0:T(8,128)(2,1)} %copy-done.6, f32[480,1536]{1,0:T(8,128)} %bitcast_convert_fusion), kind=kOutput, calls=%fused_computation.19 | convolution fusion | flops 442736640 | bytes 5242880 | tf_op jit(solution)/shard_map/dot_general | solution.py:20
  101.9 1.6 %maximum_bitcast_fusion = f32[1,3,256,768]{3,2,1,0:T(8,128)} fusion(f32[1,256,768]{2,1,0:T(8,128)S(1)} %convolution_bitcast_fusion, f32[1,256,768]{2,1,0:T(8,128)S(1)} %convolution_bitcast_fusion.1, f32[1,256,768]{2,1,0:T(8,128)S(1)} %convolution_bitcast_fusion.2), kind=kLoop, calls=%fused_computation.6 | loop fusion | flops 1179648 | bytes 4718592 | tf_op jit(solution)/shard_map/broadcast_in_dim | solution.py:106
  103.5 1.1 copy-done.5
  104.6 3.7 %fusion.1 = f32[480,1024]{1,0:T(8,128)} fusion(bf16[480,768]{1,0:T(8,128)(2,1)S(1)} %copy-done.5, bf16[1,1024,768]{2,1,0:T(8,128)(2,1)} %all-gather.6.cloned.1.call-done), kind=kOutput, calls=%fused_computation.10 | convolution fusion | flops 754974720 | bytes 4276224 | tf_op jit(solution)/shard_map/dot_general | solution.py:26
  108.3 3.6 %add_convert_fusion = bf16[480,1024]{1,0:T(8,128)(2,1)S(1)} fusion(f32[480,1024]{1,0:T(8,128)} %fusion.1, bf16[480,768]{1,0:T(8,128)(2,1)S(1)} %get-tuple-element.4, bf16[1,1024,768]{2,1,0:T(8,128)(2,1)} %all-gather.8.cloned.1.call-done), kind=kOutput, calls=%fused_computation.8 | convolution fusion | flops 755957760 | bytes 5259264 | tf_op jit(solution)/shard_map/dot_general | solution.py:26
  111.9 1.2 reshape.92
  113.1 4.5 %all-to-all-start.1 = ((bf16[16,30,1024]{2,1,0:T(8,128)(2,1)}), bf16[16,30,1024]{2,1,0:T(8,128)(2,1)S(1)}, u32[]{:S(2)}, u32[]{:S(2)}) async-start(bf16[16,30,1024]{2,1,0:T(8,128)(2,1)} %reshape.92), calls=%async_computation.1 | async-start | bytes 2097152 | tf_op jit(solution)/shard_map/all_to_all | solution.py:107
  117.7 0.2 reshape.113
  118.0 24.6 %all-to-all-done.1 = bf16[16,30,1024]{2,1,0:T(8,128)(2,1)S(1)} async-done(((bf16[16,30,1024]{2,1,0:T(8,128)(2,1)}), bf16[16,30,1024]{2,1,0:T(8,128)(2,1)S(1)}, u32[]{:S(2)}, u32[]{:S(2)}) %all-to-all-start.1) | async-done | bytes 983072 | tf_op jit(solution)/shard_map/all_to_all | solution.py:107
  142.6 0.3 reshape.93
  142.8 2.1 %gather_fusion.2 = bf16[384,1024]{1,0:T(8,128)(2,1)S(1)} fusion(bf16[480,1024]{1,0:T(8,128)(2,1)S(1)} %reshape.93, s32[1024]{0:T(1024)S(1)} %pad_clamp_fusion), kind=kCustom, calls=%fused_computation.2 | custom fusion | bytes 1574400 | tf_op jit(solution)/shard_map/gather | solution.py:115
  144.9 0.5 reshape.116
  145.4 2.1 %reduce_sum.32 = bf16[128,1024]{1,0:T(8,128)(2,1)} reduce(bf16[128,3,1024]{2,1,0:T(4,128)(2,1)S(1)} %reshape.116, bf16[]{:T(256)} %constant.47.clone.1), dimensions={1}, to_apply=%region_5.6 | reduce | flops 262144 | bytes 1048578 | tf_op jit(solution)/shard_map/reduce_sum | solution.py:115
  (35 shorter events, 0.7 us)
Async XLA Ops:
  7.2 9.9 %copy-start = (bf16[128,1024]{1,0:T(8,128)(2,1)S(1)}, bf16[128,1024]{1,0:T(8,128)(2,1)}, u32[]{:S(2)}) copy-start(bf16[128,1024]{1,0:T(8,128)(2,1)} %param.10) | copy-start | bytes 786436
  7.2 86.2 %all-gather.4.cloned.1.call-start = ((), (), s32[]{:S(2)}) async-start(), calls=%async_computation.4 | async-start | bytes 2359296 | tf_op jit(solution)/shard_map/all_gather | solution.py:81
  19.8 1.5 copy-start.2
  24.1 1.5 copy-start.1
  31.9 31.5 %all-to-all-start.2 = ((bf16[16,30,1024]{2,1,0:T(8,128)(2,1)}), bf16[16,30,1024]{2,1,0:T(8,128)(2,1)S(1)}, u32[]{:S(2)}, u32[]{:S(2)}) async-start(bf16[16,30,1024]{2,1,0:T(8,128)(2,1)} %get-tuple-element.6), calls=%async_computation.2 | async-start | bytes 2097152 | tf_op jit(solution)/shard_map/all_to_all | solution.py:64
  38.5 29.7 %copy-start.7 = (bf16[1,512,256]{2,1,0:T(8,128)(2,1)S(1)}, bf16[1,512,256]{2,1,0:T(8,128)(2,1)}, u32[]{:S(2)}) copy-start(bf16[1,512,256]{2,1,0:T(8,128)(2,1)} %param.17) | copy-start | bytes 786436
  38.5 65.1 %all-gather.6.cloned.1.call-start = ((), (), s32[]{:S(2)}) async-start(), calls=%async_computation.5 | async-start | bytes 2359296 | tf_op jit(solution)/shard_map/all_gather | solution.py:97
  63.4 29.7 %all-to-all-start = ((bf16[16,30,1024]{2,1,0:T(8,128)(2,1)}), bf16[16,30,1024]{2,1,0:T(8,128)(2,1)S(1)}, u32[]{:S(2)}, u32[]{:S(2)}) async-start(bf16[16,30,1024]{2,1,0:T(8,128)(2,1)} %get-tuple-element.7), calls=%async_computation | async-start | bytes 2097152 | tf_op jit(solution)/shard_map/all_to_all | solution.py:71
  68.1 40.1 %all-gather.8.cloned.1.call-start = ((), (), s32[]{:S(2)}) async-start(), calls=%async_computation.6 | async-start | bytes 2359296 | tf_op jit(solution)/shard_map/all_gather | solution.py:97
  68.2 7.6 %collective-permute-start = (bf16[1,512,256]{2,1,0:T(8,128)(2,1)S(1)}, bf16[1,512,256]{2,1,0:T(8,128)(2,1)}, u32[]{:S(2)}, u32[]{:S(2)}) collective-permute-start(bf16[1,512,256]{2,1,0:T(8,128)(2,1)S(1)} %copy-done.7), channel_id=1, source_target_pairs={{0,16},{16,0},{1,17},{17,1},{2,18},{18,2},{3,19},{19,3},{4,20},{20... | collective-permute-start | bytes 786440 | tf_op jit(solution)/shard_map/ppermute | solution.py:12
  68.9 78.6 %reduce-scatter.2.cloned.1.call-start = ((), (), s32[]{:S(2)}) async-start(), calls=%async_computation.7 | async-start | bytes 3538944 | tf_op jit(solution)/shard_map/reduce_scatter | solution.py:106
  78.3 2.9 %copy-start.6 = (bf16[1024,256]{1,0:T(8,128)(2,1)}, bf16[1024,256]{1,0:T(8,128)(2,1)S(1)}, u32[]{:S(2)}) copy-start(bf16[1024,256]{1,0:T(8,128)(2,1)S(1)} %fusion.9) | copy-start | bytes 1572868
  93.4 3.9 %copy-start.3 = (bf16[480,1024]{1,0:T(8,128)(2,1)}, bf16[480,1024]{1,0:T(8,128)(2,1)S(1)}, u32[]{:S(2)}) copy-start(bf16[480,1024]{1,0:T(8,128)(2,1)S(1)} %reshape.91) | copy-start | bytes 2949124
  97.3 0.9 copy-start.4
  103.5 1.1 copy-start.5
  113.1 29.4 %all-to-all-start.1 = ((bf16[16,30,1024]{2,1,0:T(8,128)(2,1)}), bf16[16,30,1024]{2,1,0:T(8,128)(2,1)S(1)}, u32[]{:S(2)}, u32[]{:S(2)}) async-start(bf16[16,30,1024]{2,1,0:T(8,128)(2,1)} %reshape.92), calls=%async_computation.1 | async-start | bytes 2097152 | tf_op jit(solution)/shard_map/all_to_all | solution.py:107
Sparse Core Ops, SparseCore 0:
  9.5 27.2 all-gather.3
  40.8 26.6 all-gather.5
  70.5 26.6 all-gather.7
  103.6 33.0 reduce-scatter.1
